TPU v7x, 32 devices: a whole 2x2x4 slice. The times are simulated.
32 devices in a mesh: dp: 4 (over y, core), vocab: 8 (over z, x).
Axes of the slice: x: 2, y: 2, z: 4, core: 2. Of those that a mesh axis runs over, the one named last changes fastest.
Arguments:
- teacher_hidden: bfloat16 [512, 16384], P('dp', 'vocab'), may hold values from -120 to 120
- student_hidden: bfloat16 [512, 4096], P('dp', 'vocab'), may hold values from -120 to 120
- teacher_weight: bfloat16 [16384, 65536], P('dp', 'vocab'), may hold values from -1 to 1
- student_weight: bfloat16 [4096, 65536], P('dp', 'vocab'), may hold values from -1 to 1
Outputs:
- kl: float32 [512], P('dp')
- loss: float32 [], replicated
All inputs are finite; a program needn't handle non-finite values.
Results may differ from a plain program's by a relative error of at most 0.0003.
Values may be sent and summed in bfloat16 or wider, within the bound.
A program may use at most 256 MiB of HBM per device.

v0:
```python
import jax
import jax.numpy as jnp
from jax import lax
from jax.sharding import PartitionSpec as P

SPAN = 240.0


def encode(block):
    mag = jnp.abs(block)
    top = jnp.max(mag, axis=1, keepdims=True)
    step = jnp.where(top > 0, SPAN / jnp.where(top > 0, top, 1.0), 0.0)
    power = jnp.exp2(mag * step - 0.5 * SPAN)
    return jnp.where(block < 0, -power, power).astype(jnp.bfloat16), top


def decode(code, top):
    value = code.astype(jnp.float32)
    mag = (jnp.log2(jnp.abs(value)) + 0.5 * SPAN) * (top * (1.0 / SPAN))
    return jnp.where(value < 0, -mag, mag)


def pair_sum(part, n_dp):
    half = part.shape[0] // 2
    return part[:half] + lax.ppermute(part[half:], "dp", [(i, i ^ 1) for i in range(n_dp)])


def encode_groups(both, n_dp, tok):
    return [encode(both[j * tok : (j + 1) * tok]) for j in range(1, n_dp // 2)]


def exchange(both, codes, n_dp, tok):
    total = both[:tok]
    for j, (code, top) in enumerate(codes, 1):
        perm = [(i, i ^ (2 * j)) for i in range(n_dp)]
        total = total + decode(lax.ppermute(code, "dp", perm), lax.ppermute(top, "dp", perm))
    return total


def shards(teacher_hidden, student_hidden, teacher_weight, student_weight):
    n_dp, n_vocab = lax.axis_size("dp"), lax.axis_size("vocab")
    tok, wide = teacher_hidden.shape
    narrow = student_hidden.shape[1]
    per, blocks = tok // n_vocab, n_vocab // n_dp
    me = lax.axis_index("dp")

    both = jnp.concatenate([teacher_hidden, student_hidden], axis=1).reshape(n_vocab, per, wide + narrow)
    both = lax.all_to_all(both, "vocab", split_axis=0, concat_axis=0, tiled=True)
    both = both.reshape(n_dp, blocks * per, wide + narrow)
    both = lax.all_to_all(both, "dp", split_axis=0, concat_axis=0, tiled=True)
    order = jnp.array(list(range(0, n_dp, 2)) + list(range(1, n_dp, 2)), jnp.int32) ^ me
    both = jnp.take(both, order, axis=0).reshape(n_dp, blocks, per, wide + narrow)
    both = both.transpose(0, 2, 1, 3)

    def gather(piece):
        full = lax.all_gather(piece, "vocab", axis=1, tiled=True)
        return full.reshape(n_dp * tok, -1)

    student_piece = both[..., wide:].reshape(n_dp, per, -1)
    teacher_piece = both[..., :wide].reshape(n_dp, per, -1)
    student_piece, teacher_piece = lax.optimization_barrier((student_piece, teacher_piece))
    student_rows, teacher_rows = gather(student_piece), gather(teacher_piece)

    def head(rows, weight, pieces):
        cols = weight.shape[1] // pieces
        out, waiting = [], []

        def finish(rows):
            both = pair_sum(waiting.pop(0), n_dp)
            rows, both, codes = lax.optimization_barrier((rows, both, encode_groups(both, n_dp, tok)))
            out.append(exchange(both, codes, n_dp, tok))
            return rows

        for i in range(pieces):
            if len(waiting) == 2:
                rows = finish(rows)
            piece = weight[:, i * cols : (i + 1) * cols]
            waiting.append(jnp.dot(rows, piece, preferred_element_type=jnp.float32))
        while waiting:
            rows = finish(rows)
        return out

    pieces = 4
    student = head(student_rows, student_weight, pieces)
    teacher = head(teacher_rows, teacher_weight, pieces)

    def top_of(parts):
        top = jnp.max(parts[0], axis=1)
        for p in parts[1:]:
            top = jnp.maximum(top, jnp.max(p, axis=1))
        return top

    t_top, s_top = top_of(teacher), top_of(student)
    t_sum = w_sum = s_sum = 0.0
    for t, s in zip(teacher, student):
        e = jnp.exp(t - t_top[:, None])
        t_sum = t_sum + jnp.sum(e, axis=1)
        w_sum = w_sum + jnp.sum(e * (t - s), axis=1)
        s_sum = s_sum + jnp.sum(jnp.exp(s - s_top[:, None]), axis=1)

    stats = lax.all_gather(jnp.stack([t_top, s_top, t_sum, w_sum, s_sum]), ("dp", "vocab"))
    stats = stats.reshape(n_dp, n_vocab, 5, tok)
    t_tops, s_tops = stats[:, :, 0], stats[:, :, 1]
    t_max, s_max = jnp.max(t_tops, axis=1), jnp.max(s_tops, axis=1)
    t_scale = jnp.exp(t_tops - t_max[:, None])
    t_total = jnp.sum(t_scale * stats[:, :, 2], axis=1)
    weighted = jnp.sum(t_scale * stats[:, :, 3], axis=1)
    s_total = jnp.sum(jnp.exp(s_tops - s_max[:, None]) * stats[:, :, 4], axis=1)
    kl = weighted / t_total - (t_max + jnp.log(t_total)) + (s_max + jnp.log(s_total))
    loss = jnp.sum(kl) / (tok * n_dp)
    return lax.dynamic_index_in_dim(kl, me, axis=0, keepdims=False), loss


def solution(mesh):
    in_specs = (P("dp", "vocab"), P("dp", "vocab"), P("dp", "vocab"), P("dp", "vocab"))
    out_specs = (P("dp"), P())
    return jax.shard_map(shards, mesh=mesh, in_specs=in_specs, out_specs=out_specs, check_vma=False)
```

profile of v0, /device:TPU:0, one launch (start us, length us, event | category | flops | bytes accessed | tf_op | source)
XLA Modules:
  0.0 353.4 jit_solution(18426221453421665546)
XLA Ops:
  8.3 24.9 %all_to_all.10 = bf16[8,16,2560]{2,1,0:T(8,128)(2,1)} all-to-all(bf16[8,16,2560]{2,1,0:T(8,128)(2,1)S(1)} %bitcast.69), channel_id=1, replica_groups=mesh['dp'=4,'vocab'=8] {'vocab'}, dimensions={0} | all-to-all | bytes 1310720 | tf_op jit(solution)/shard_map/all_to_all | solution.py:48
  33.2 3.5 all-to-all-start.1
  36.8 10.1 %all-to-all-done.1 = bf16[4,32,2560]{2,1,0:T(8,128)(2,1)S(1)} async-done(((bf16[4,32,2560]{2,1,0:T(8,128)(2,1)}), bf16[4,32,2560]{2,1,0:T(8,128)(2,1)S(1)}, u32[]{:S(2)}, u32[]{:S(2)}) %all-to-all-start.1) | async-done | bytes 655392 | tf_op jit(solution)/shard_map/all_to_all | solution.py:50
  49.2 38.1 %all-gather.7.cloned.1.call-done = bf16[4,128,1024]{2,1,0:T(8,128)(2,1)} async-done(((bf16[4,16,1024]{2,1,0:T(8,128)(2,1)}), bf16[4,128,1024]{2,1,0:T(8,128)(2,1)}) %all-gather.7.cloned.1.call-update) | async-done | bytes 1048592 | tf_op jit(solution)/shard_map/all_gather | solution.py:56
  87.3 4.8 %fusion.14 = f32[512,2048]{1,0:T(8,128)S(1)} fusion(bf16[512,1024]{1,0:T(8,128)(2,1)} %bitcast.95, bf16[1024,8192]{1,0:T(8,128)(2,1)} %param.8), kind=kOutput, calls=%fused_computation.15 | convolution fusion | flops 2147483648 | bytes 9437184 | tf_op jit(solution)/shard_map/dot_general | solution.py:78
  92.4 1.7 copy-done.9
  94.2 4.5 %fusion.12 = f32[512,2048]{1,0:T(8,128)S(1)} fusion(bf16[512,1024]{1,0:T(8,128)(2,1)S(1)} %bitcast.97, bf16[1024,8192]{1,0:T(8,128)(2,1)} %param.8), kind=kOutput, calls=%fused_computation.13 | convolution fusion | flops 2147483648 | bytes 9437184 | tf_op jit(solution)/shard_map/dot_general | solution.py:78
  98.7 1.6 slice.208
  101.9 2.6 slice_add_fusion.3
  105.9 1.9 slice_add_fusion.2
  109.9 4.5 %fusion.8 = f32[512,2048]{1,0:T(8,128)S(1)} fusion(bf16[512,1024]{1,0:T(8,128)(2,1)S(1)} %bitcast.98, bf16[1024,8192]{1,0:T(8,128)(2,1)} %param.8), kind=kOutput, calls=%fused_computation.9 | convolution fusion | flops 2147483648 | bytes 9437184 | tf_op jit(solution)/shard_map/dot_general | solution.py:78
  114.4 1.5 slice.214
  119.4 4.9 %fusion.10 = f32[512,2048]{1,0:T(8,128)S(1)} fusion(bf16[512,1024]{1,0:T(8,128)(2,1)} %bitcast.96, bf16[1024,8192]{1,0:T(8,128)(2,1)} %param.8), kind=kOutput, calls=%fused_computation.11 | convolution fusion | flops 2147483648 | bytes 9437184 | tf_op jit(solution)/shard_map/dot_general | solution.py:78
  124.3 1.6 collective-permute-start.14
  126.7 7.1 %collective-permute-done.14 = f32[128,1]{0,1:T(1,128)S(1)} collective-permute-done((f32[128,1]{0,1:T(1,128)S(1)}, f32[128,1]{0,1:T(1,128)S(1)}, u32[]{:S(2)}, u32[]{:S(2)}) %collective-permute-start.14) | collective-permute-done | bytes 544 | tf_op jit(solution)/shard_map/ppermute | solution.py:36
  134.3 9.5 %collective-permute-done.13 = bf16[128,2048]{1,0:T(8,128)(2,1)S(1)} collective-permute-done((bf16[128,2048]{1,0:T(8,128)(2,1)}, bf16[128,2048]{1,0:T(8,128)(2,1)S(1)}, u32[]{:S(2)}, u32[]{:S(2)}) %collective-permute-start.13) | collective-permute-done | bytes 524320 | tf_op jit(solution)/shard_map/ppermute | solution.py:36
  145.4 1.9 slice_add_fusion
  149.2 1.5 collective-permute-start.22
  155.8 8.5 %collective-permute-done.20 = f32[128,1]{0,1:T(1,128)S(1)} collective-permute-done((f32[128,1]{0,1:T(1,128)S(1)}, f32[128,1]{0,1:T(1,128)S(1)}, u32[]{:S(2)}, u32[]{:S(2)}) %collective-permute-start.20) | collective-permute-done | bytes 544 | tf_op jit(solution)/shard_map/ppermute | solution.py:36
  164.3 9.2 %all-gather.5.cloned.1.call-done = bf16[4,128,4096]{2,1,0:T(8,128)(2,1)} async-done(((bf16[4,16,4096]{2,1,0:T(8,128)(2,1)}), bf16[4,128,4096]{2,1,0:T(8,128)(2,1)}) %all-gather.5.cloned.1.call-update) | async-done | bytes 4194320 | tf_op jit(solution)/shard_map/all_gather | solution.py:56
  173.5 12.8 %fusion.4 = f32[512,2048]{1,0:T(8,128)S(1)} fusion(bf16[512,4096]{1,0:T(8,128)(2,1)} %bitcast.91, bf16[4096,8192]{1,0:T(8,128)(2,1)} %param.7), kind=kOutput, calls=%fused_computation.5 | convolution fusion | flops 8589934592 | bytes 25165824 | tf_op jit(solution)/shard_map/dot_general | solution.py:78
  186.6 12.9 %fusion.6 = f32[512,2048]{1,0:T(8,128)S(1)} fusion(bf16[512,4096]{1,0:T(8,128)(2,1)} %bitcast.92, bf16[4096,8192]{1,0:T(8,128)(2,1)} %param.7), kind=kOutput, calls=%fused_computation.7 | convolution fusion | flops 8589934592 | bytes 25165824 | tf_op jit(solution)/shard_map/dot_general | solution.py:78
  200.3 1.6 fusion.83
  201.9 1.6 fusion.81
  208.2 12.8 %fusion = f32[512,2048]{1,0:T(8,128)S(1)} fusion(bf16[512,4096]{1,0:T(8,128)(2,1)} %bitcast.93, bf16[4096,8192]{1,0:T(8,128)(2,1)} %param.7), kind=kOutput, calls=%fused_computation.1 | convolution fusion | flops 8589934592 | bytes 25165824 | tf_op jit(solution)/shard_map/dot_general | solution.py:78
  221.3 13.1 %fusion.2 = f32[512,2048]{1,0:T(8,128)S(1)} fusion(bf16[512,4096]{1,0:T(8,128)(2,1)} %bitcast.94, bf16[4096,8192]{1,0:T(8,128)(2,1)} %param.7), kind=kOutput, calls=%fused_computation.3 | convolution fusion | flops 8589934592 | bytes 25165824 | tf_op jit(solution)/shard_map/dot_general | solution.py:78
  234.4 1.6 collective-permute-start.2
  238.6 11.6 %collective-permute-done.1 = bf16[128,2048]{1,0:T(8,128)(2,1)S(1)} collective-permute-done((bf16[128,2048]{1,0:T(8,128)(2,1)}, bf16[128,2048]{1,0:T(8,128)(2,1)S(1)}, u32[]{:S(2)}, u32[]{:S(2)}) %collective-permute-start.1) | collective-permute-done | bytes 524320 | tf_op jit(solution)/shard_map/ppermute | solution.py:36
  256.7 10.4 %collective-permute-done.8 = f32[128,1]{0,1:T(1,128)S(1)} collective-permute-done((f32[128,1]{0,1:T(1,128)S(1)}, f32[128,1]{0,1:T(1,128)S(1)}, u32[]{:S(2)}, u32[]{:S(2)}) %collective-permute-start.8) | collective-permute-done | bytes 544 | tf_op jit(solution)/shard_map/ppermute | solution.py:36
  267.7 8.7 %collective-permute-done.7 = bf16[128,2048]{1,0:T(8,128)(2,1)S(1)} collective-permute-done((bf16[128,2048]{1,0:T(8,128)(2,1)S(1)}, bf16[128,2048]{1,0:T(8,128)(2,1)S(1)}, u32[]{:S(2)}, u32[]{:S(2)}) %collective-permute-start.7) | collective-permute-done | bytes 524320 | tf_op jit(solution)/shard_map/ppermute | solution.py:36
  277.0 1.9 multiply_reduce_fusion
  278.9 64.5 %all-gather.1 = f32[32,5,128]{2,1,0:T(8,128)S(1)} all-gather(f32[1,5,128]{2,1,0:T(8,128)S(1)} %bitcast.80), channel_id=2, replica_groups=mesh['dp'=4,'vocab'=8] {'dp','vocab'}, dimensions={0}, use_global_device_ids=true | all-gather | bytes 84480 | tf_op jit(solution)/shard_map/all_gather | solution.py:101
  (138 shorter events, 39.5 us)
Async XLA Ops:
  7.2 29.6 %copy-start.10 = (s32[4]{0:T(128)S(1)}, s32[4]{0:T(128)}, u32[]{:S(2)}) copy-start(s32[4]{0:T(128)} %constant.57.clone) | copy-start | bytes 52
  33.2 13.7 %all-to-all-start.1 = ((bf16[4,32,2560]{2,1,0:T(8,128)(2,1)}), bf16[4,32,2560]{2,1,0:T(8,128)(2,1)S(1)}, u32[]{:S(2)}, u32[]{:S(2)}) async-start(bf16[4,32,2560]{2,1,0:T(8,128)(2,1)} %bitcast.1), calls=%async_computation.1 | async-start | bytes 1310720 | tf_op jit(solution)/shard_map/all_to_all | solution.py:50
  36.7 50.6 %all-gather.7.cloned.1.call-start = ((), (), s32[]{:S(2)}) async-start(), calls=%async_computation.3 | async-start | bytes 1179648 | tf_op jit(solution)/shard_map/all_gather | solution.py:56
  49.2 124.3 %all-gather.5.cloned.1.call-start = ((), (), s32[]{:S(2)}) async-start(), calls=%async_computation.2 | async-start | bytes 4718592 | tf_op jit(solution)/shard_map/all_gather | solution.py:56
  94.1 7.7 %collective-permute-start.12 = (f32[256,2048]{1,0:T(8,128)S(1)}, f32[256,2048]{1,0:T(8,128)}, u32[]{:S(2)}, u32[]{:S(2)}) collective-permute-start(f32[256,2048]{1,0:T(8,128)S(1)} %slice.205), channel_id=1, source_target_pairs={{0,8},{8,0},{16,24},{24,16},{1,9},{9,1},{17,25},{25,17},{2,10},{10... | collective-permute-start | bytes 6291464 | tf_op jit(solution)/shard_map/ppermute | solution.py:25
  101.3 4.6 %collective-permute-start.15 = (f32[256,2048]{1,0:T(8,128)}, f32[256,2048]{1,0:T(8,128)}, u32[]{:S(2)}, u32[]{:S(2)}) collective-permute-start(f32[256,2048]{1,0:T(8,128)} %slice.208), channel_id=1, source_target_pairs={{0,8},{8,0},{16,24},{24,16},{1,9},{9,1},{17,25},{25,17},{2,10},{10... | collective-permute-start | bytes 6291464 | tf_op jit(solution)/shard_map/ppermute | solution.py:25
  101.8 4.1 %copy-start.8 = (f32[512,2048]{1,0:T(8,128)S(1)}, f32[512,2048]{1,0:T(8,128)}, u32[]{:S(2)}) copy-start(f32[512,2048]{1,0:T(8,128)} %copy-done.7) | copy-start | bytes 12582916
  117.0 28.3 %collective-permute-start.21 = (f32[256,2048]{1,0:T(8,128)}, f32[256,2048]{1,0:T(8,128)}, u32[]{:S(2)}, u32[]{:S(2)}) collective-permute-start(f32[256,2048]{1,0:T(8,128)} %slice.214), channel_id=1, source_target_pairs={{0,8},{8,0},{16,24},{24,16},{1,9},{9,1},{17,25},{25,17},{2,10},{10... | collective-permute-start | bytes 6291464 | tf_op jit(solution)/shard_map/ppermute | solution.py:25
  117.4 9.2 %collective-permute-start.17 = (f32[128,1]{0,1:T(1,128)S(1)}, f32[128,1]{0,1:T(1,128)S(1)}, u32[]{:S(2)}, u32[]{:S(2)}) collective-permute-start(f32[128,1]{0,1:T(1,128)S(1)} %bitcast.86), channel_id=1, source_target_pairs={{0,16},{8,24},{16,0},{24,8},{1,17},{9,25},{17,1},{25,9},{2,18},{10... | collective-permute-start | bytes 1544 | tf_op jit(solution)/shard_map/ppermute | solution.py:36
  118.9 14.9 %collective-permute-start.16 = (bf16[128,2048]{1,0:T(8,128)(2,1)S(1)}, bf16[128,2048]{1,0:T(8,128)(2,1)S(1)}, u32[]{:S(2)}, u32[]{:S(2)}) collective-permute-start(bf16[128,2048]{1,0:T(8,128)(2,1)S(1)} %fusion.58), channel_id=1, source_target_pairs={{0,16},{8,24},{16,0},{24,8},{1,17},{9,25},{17,1},{25,9},{2,18},{10... | collective-permute-start | bytes 1572872 | tf_op jit(solution)/shard_map/ppermute | solution.py:36
  124.3 9.5 %copy-start.1 = (f32[256,2048]{1,0:T(8,128)S(1)}, f32[256,2048]{1,0:T(8,128)}, u32[]{:S(2)}) copy-start(f32[256,2048]{1,0:T(8,128)} %copy-done) | copy-start | bytes 6291460
  124.3 9.5 %collective-permute-start.14 = (f32[128,1]{0,1:T(1,128)S(1)}, f32[128,1]{0,1:T(1,128)S(1)}, u32[]{:S(2)}, u32[]{:S(2)}) collective-permute-start(f32[128,1]{0,1:T(1,128)S(1)} %bitcast.83), channel_id=1, source_target_pairs={{0,16},{8,24},{16,0},{24,8},{1,17},{9,25},{17,1},{25,9},{2,18},{10... | collective-permute-start | bytes 1544 | tf_op jit(solution)/shard_map/ppermute | solution.py:36
  125.9 18.0 %collective-permute-start.13 = (bf16[128,2048]{1,0:T(8,128)(2,1)}, bf16[128,2048]{1,0:T(8,128)(2,1)S(1)}, u32[]{:S(2)}, u32[]{:S(2)}) collective-permute-start(bf16[128,2048]{1,0:T(8,128)(2,1)} %fusion.56), channel_id=1, source_target_pairs={{0,16},{8,24},{16,0},{24,8},{1,17},{9,25},{17,1},{25,9},{2,18},{10... | collective-permute-start | bytes 1572872 | tf_op jit(solution)/shard_map/ppermute | solution.py:36
  126.6 24.1 %collective-permute-start.18 = (f32[256,2048]{1,0:T(8,128)S(1)}, f32[256,2048]{1,0:T(8,128)S(1)}, u32[]{:S(2)}, u32[]{:S(2)}) collective-permute-start(f32[256,2048]{1,0:T(8,128)S(1)} %slice.211), channel_id=1, source_target_pairs={{0,8},{8,0},{16,24},{24,16},{1,9},{9,1},{17,25},{25,17},{2,10},{10... | collective-permute-start | bytes 6291464 | tf_op jit(solution)/shard_map/ppermute | solution.py:25
  133.8 11.6 %copy-start.6 = (f32[512,2048]{1,0:T(8,128)S(1)}, f32[512,2048]{1,0:T(8,128)}, u32[]{:S(2)}) copy-start(f32[512,2048]{1,0:T(8,128)} %copy-done.5) | copy-start | bytes 12582916
  148.6 7.1 %collective-permute-start.23 = (f32[128,1]{0,1:T(1,128)S(1)}, f32[128,1]{0,1:T(1,128)S(1)}, u32[]{:S(2)}, u32[]{:S(2)}) collective-permute-start(f32[128,1]{0,1:T(1,128)S(1)} %bitcast.87), channel_id=1, source_target_pairs={{0,16},{8,24},{16,0},{24,8},{1,17},{9,25},{17,1},{25,9},{2,18},{10... | collective-permute-start | bytes 1544 | tf_op jit(solution)/shard_map/ppermute | solution.py:36
  149.2 51.1 %collective-permute-start.22 = (bf16[128,2048]{1,0:T(8,128)(2,1)}, bf16[128,2048]{1,0:T(8,128)(2,1)}, u32[]{:S(2)}, u32[]{:S(2)}) collective-permute-start(bf16[128,2048]{1,0:T(8,128)(2,1)} %fusion.62), channel_id=1, source_target_pairs={{0,16},{8,24},{16,0},{24,8},{1,17},{9,25},{17,1},{25,9},{2,18},{10... | collective-permute-start | bytes 1572872 | tf_op jit(solution)/shard_map/ppermute | solution.py:36
  153.7 10.5 %collective-permute-start.20 = (f32[128,1]{0,1:T(1,128)S(1)}, f32[128,1]{0,1:T(1,128)S(1)}, u32[]{:S(2)}, u32[]{:S(2)}) collective-permute-start(f32[128,1]{0,1:T(1,128)S(1)} %bitcast.89), channel_id=1, source_target_pairs={{0,16},{8,24},{16,0},{24,8},{1,17},{9,25},{17,1},{25,9},{2,18},{10... | collective-permute-start | bytes 1544 | tf_op jit(solution)/shard_map/ppermute | solution.py:36
  154.2 47.7 %collective-permute-start.19 = (bf16[128,2048]{1,0:T(8,128)(2,1)}, bf16[128,2048]{1,0:T(8,128)(2,1)}, u32[]{:S(2)}, u32[]{:S(2)}) collective-permute-start(bf16[128,2048]{1,0:T(8,128)(2,1)} %fusion.60), channel_id=1, source_target_pairs={{0,16},{8,24},{16,0},{24,8},{1,17},{9,25},{17,1},{25,9},{2,18},{10... | collective-permute-start | bytes 1572872 | tf_op jit(solution)/shard_map/ppermute | solution.py:36
  186.5 17.0 %collective-permute-start.3 = (f32[256,2048]{1,0:T(8,128)S(1)}, f32[256,2048]{1,0:T(8,128)S(1)}, u32[]{:S(2)}, u32[]{:S(2)}) collective-permute-start(f32[256,2048]{1,0:T(8,128)S(1)} %slice.196), channel_id=1, source_target_pairs={{0,8},{8,0},{16,24},{24,16},{1,9},{9,1},{17,25},{25,17},{2,10},{10... | collective-permute-start | bytes 6291464 | tf_op jit(solution)/shard_map/ppermute | solution.py:25
  199.7 4.7 %collective-permute-start = (f32[256,2048]{1,0:T(8,128)S(1)}, f32[256,2048]{1,0:T(8,128)S(1)}, u32[]{:S(2)}, u32[]{:S(2)}) collective-permute-start(f32[256,2048]{1,0:T(8,128)S(1)} %slice.193), channel_id=1, source_target_pairs={{0,8},{8,0},{16,24},{24,16},{1,9},{9,1},{17,25},{25,17},{2,10},{10... | collective-permute-start | bytes 6291464 | tf_op jit(solution)/shard_map/ppermute | solution.py:25
  206.1 30.6 %collective-permute-start.5 = (f32[128,1]{0,1:T(1,128)S(1)}, f32[128,1]{0,1:T(1,128)S(1)}, u32[]{:S(2)}, u32[]{:S(2)}) collective-permute-start(f32[128,1]{0,1:T(1,128)S(1)} %bitcast.84), channel_id=1, source_target_pairs={{0,16},{8,24},{16,0},{24,8},{1,17},{9,25},{17,1},{25,9},{2,18},{10... | collective-permute-start | bytes 1544 | tf_op jit(solution)/shard_map/ppermute | solution.py:36
  207.6 30.4 %collective-permute-start.4 = (bf16[128,2048]{1,0:T(8,128)(2,1)S(1)}, bf16[128,2048]{1,0:T(8,128)(2,1)S(1)}, u32[]{:S(2)}, u32[]{:S(2)}) collective-permute-start(bf16[128,2048]{1,0:T(8,128)(2,1)S(1)} %fusion.50), channel_id=1, source_target_pairs={{0,16},{8,24},{16,0},{24,8},{1,17},{9,25},{17,1},{25,9},{2,18},{10... | collective-permute-start | bytes 1572872 | tf_op jit(solution)/shard_map/ppermute | solution.py:36
  221.2 29.5 %collective-permute-start.9 = (f32[256,2048]{1,0:T(8,128)S(1)}, f32[256,2048]{1,0:T(8,128)S(1)}, u32[]{:S(2)}, u32[]{:S(2)}) collective-permute-start(f32[256,2048]{1,0:T(8,128)S(1)} %slice.202), channel_id=1, source_target_pairs={{0,8},{8,0},{16,24},{24,16},{1,9},{9,1},{17,25},{25,17},{2,10},{10... | collective-permute-start | bytes 6291464 | tf_op jit(solution)/shard_map/ppermute | solution.py:25
  234.4 3.6 %collective-permute-start.2 = (f32[128,1]{0,1:T(1,128)S(1)}, f32[128,1]{0,1:T(1,128)S(1)}, u32[]{:S(2)}, u32[]{:S(2)}) collective-permute-start(f32[128,1]{0,1:T(1,128)S(1)} %bitcast.85), channel_id=1, source_target_pairs={{0,16},{8,24},{16,0},{24,8},{1,17},{9,25},{17,1},{25,9},{2,18},{10... | collective-permute-start | bytes 1544 | tf_op jit(solution)/shard_map/ppermute | solution.py:36
  236.0 14.2 %collective-permute-start.1 = (bf16[128,2048]{1,0:T(8,128)(2,1)}, bf16[128,2048]{1,0:T(8,128)(2,1)S(1)}, u32[]{:S(2)}, u32[]{:S(2)}) collective-permute-start(bf16[128,2048]{1,0:T(8,128)(2,1)} %fusion.48), channel_id=1, source_target_pairs={{0,16},{8,24},{16,0},{24,8},{1,17},{9,25},{17,1},{25,9},{2,18},{10... | collective-permute-start | bytes 1572872 | tf_op jit(solution)/shard_map/ppermute | solution.py:36
  236.7 17.0 %collective-permute-start.6 = (f32[256,2048]{1,0:T(8,128)S(1)}, f32[256,2048]{1,0:T(8,128)S(1)}, u32[]{:S(2)}, u32[]{:S(2)}) collective-permute-start(f32[256,2048]{1,0:T(8,128)S(1)} %slice.199), channel_id=1, source_target_pairs={{0,8},{8,0},{16,24},{24,16},{1,9},{9,1},{17,25},{25,17},{2,10},{10... | collective-permute-start | bytes 6291464 | tf_op jit(solution)/shard_map/ppermute | solution.py:25
  251.6 5.1 %collective-permute-start.11 = (f32[128,1]{0,1:T(1,128)S(1)}, f32[128,1]{0,1:T(1,128)S(1)}, u32[]{:S(2)}, u32[]{:S(2)}) collective-permute-start(f32[128,1]{0,1:T(1,128)S(1)} %bitcast.88), channel_id=1, source_target_pairs={{0,16},{8,24},{16,0},{24,8},{1,17},{9,25},{17,1},{25,9},{2,18},{10... | collective-permute-start | bytes 1544 | tf_op jit(solution)/shard_map/ppermute | solution.py:36
  252.3 14.9 %collective-permute-start.10 = (bf16[128,2048]{1,0:T(8,128)(2,1)S(1)}, bf16[128,2048]{1,0:T(8,128)(2,1)S(1)}, u32[]{:S(2)}, u32[]{:S(2)}) collective-permute-start(bf16[128,2048]{1,0:T(8,128)(2,1)S(1)} %fusion.54), channel_id=1, source_target_pairs={{0,16},{8,24},{16,0},{24,8},{1,17},{9,25},{17,1},{25,9},{2,18},{10... | collective-permute-start | bytes 1572872 | tf_op jit(solution)/shard_map/ppermute | solution.py:36
  254.7 12.5 %collective-permute-start.8 = (f32[128,1]{0,1:T(1,128)S(1)}, f32[128,1]{0,1:T(1,128)S(1)}, u32[]{:S(2)}, u32[]{:S(2)}) collective-permute-start(f32[128,1]{0,1:T(1,128)S(1)} %bitcast.90), channel_id=1, source_target_pairs={{0,16},{8,24},{16,0},{24,8},{1,17},{9,25},{17,1},{25,9},{2,18},{10... | collective-permute-start | bytes 1544 | tf_op jit(solution)/shard_map/ppermute | solution.py:36
  255.3 21.1 %collective-permute-start.7 = (bf16[128,2048]{1,0:T(8,128)(2,1)S(1)}, bf16[128,2048]{1,0:T(8,128)(2,1)S(1)}, u32[]{:S(2)}, u32[]{:S(2)}) collective-permute-start(bf16[128,2048]{1,0:T(8,128)(2,1)S(1)} %fusion.52), channel_id=1, source_target_pairs={{0,16},{8,24},{16,0},{24,8},{1,17},{9,25},{17,1},{25,9},{2,18},{10... | collective-permute-start | bytes 1572872 | tf_op jit(solution)/shard_map/ppermute | solution.py:36
  267.2 9.8 %copy-start.4 = (f32[128,2048]{1,0:T(8,128)S(1)}, f32[128,2048]{1,0:T(8,128)}, u32[]{:S(2)}) copy-start(f32[128,2048]{1,0:T(8,128)} %get-tuple-element.90) | copy-start | bytes 3145732
  (8 other events, 16.1 us)
Sparse Core Ops, SparseCore 0:
  49.3 37.9 all-gather.6
  102.0 71.4 all-gather.4
where the time goes:
time: 354 us; the launch traced here: 353 us
  waiting for transfers between devices  115 us (32%)
  blocking collectives  89.4 us (25%)
  matrix products  70.4 us (20%)
  other arithmetic  27.3 us (8%)
  starting transfers between devices  21.7 us (6%)
  between operations  16.4 us (5%)
  local copies, waits for them, and re-layouts  13.6 us (4%)
    dot_general x8, matrix products, head(): waiting.append(jnp.dot(rows, piece, preferred_element_type=jnp.float32))  70.4 us
    all_gather x1, blocking collectives, shards(): lax.all_gather(jnp.stack([t_top, s_top, t_sum, w_sum, s_sum]), ('dp', 'vo...  64.5 us
    all_gather x2, waiting for transfers between devices, gather(): full = lax.all_gather(piece, 'vocab', axis=1, tiled=True)  47.3 us
    ppermute x8, waiting for transfers between devices, exchange(): lax.ppermute(code, 'dp', perm)  29.9 us
    ppermute x8, waiting for transfers between devices, exchange(): lax.ppermute(top, 'dp', perm)  27.2 us
    all_to_all x1, blocking collectives, shards(): lax.all_to_all(both, 'vocab', split_axis=0, concat_axis=0, tiled=True)  24.9 us
    all_to_all x1, waiting for transfers between devices, shards(): both = lax.all_to_all(both, 'dp', split_axis=0, concat_axis=0, tiled=True)  10.1 us
    ppermute x8, starting transfers between devices, exchange(): lax.ppermute(top, 'dp', perm)  8.37 us
  transfers between devices with their start and end apart: 27, of which 11 were waited for; matrix products, arithmetic and copies ran while one was open for 26% of the time, Pallas kernels for 0%

commit v1 on v0

v1 whole, which is shorter than its diff:
```python
import functools

import jax
import jax.numpy as jnp
from jax import lax
from jax.experimental import pallas as pl
from jax.experimental.pallas import tpu as pltpu
from jax.sharding import PartitionSpec as P

MESH = pl.DeviceIdType.MESH
SPAN = 240.0
LANES = 128
SLOTS = 3
HOP = 3
SPACE = 4


def encode(block):
    mag = jnp.abs(block)
    top = jnp.max(mag, axis=1, keepdims=True)
    step = jnp.where(top > 0, SPAN / jnp.where(top > 0, top, 1.0), 0.0)
    power = jnp.exp2(mag * step - 0.5 * SPAN)
    return jnp.where(block < 0, -power, power).astype(jnp.bfloat16), top


def decode(code, scale):
    value = code.astype(jnp.float32)
    mag = (jnp.log2(jnp.abs(value)) + 0.5 * SPAN) * scale
    return jnp.where(value < 0, -mag, mag)


def kernel(
    n_dp, n_vocab, cols,
    th_ref, sh_ref, tw_ref, sw_ref, kl_ref, loss_ref,
    hid_t, hid_s, wt, ws, part, pair_a, pair_b, code_out, code_in, top_out, top_in, run,
    st_out, st_in, ls_out, ls_in,
    g_recv, g_send, src_send, w_sem, d_send, d_recv, y_send, y_recv, st_send, st_recv, ls_send, ls_recv,
):
    tok, wide = th_ref.shape
    narrow = sh_ref.shape[1]
    half = tok // 2
    n_y = n_dp // 2
    per = n_vocab // n_dp
    n = tw_ref.shape[1] // cols
    passes = 2 * (n_y - 1)
    n_a = passes * n
    total = n_a + n
    n_slots = 4 * n_y

    d, v = lax.axis_index("dp"), lax.axis_index("vocab")
    y, core = d // 2, lax.rem(d, 2)
    row, col = v // per, lax.rem(v, per)

    def remote(src, dst, send, recv, dp, vocab):
        return pltpu.make_async_remote_copy(
            src_ref=src, dst_ref=dst, send_sem=send, recv_sem=recv,
            device_id={"dp": dp, "vocab": vocab}, device_id_type=MESH,
        )

    def weight_copies(g):
        at = pl.ds(pl.multiple_of(lax.rem(g, n) * cols, LANES), cols)
        slot = lax.rem(g, SLOTS)
        return (
            pltpu.make_async_copy(tw_ref.at[:, at], wt.at[slot], w_sem.at[slot, 0]),
            pltpu.make_async_copy(sw_ref.at[:, at], ws.at[slot], w_sem.at[slot, 1]),
        )

    def weights_start(g):
        for copy in weight_copies(g):
            copy.start()

    for g in range(SLOTS - 1):
        weights_start(jnp.int32(g))

    barrier = pltpu.get_barrier_semaphore()
    for o in range(1, n_dp):
        pl.semaphore_signal(barrier, inc=1, device_id={"dp": lax.rem(d + o, n_dp), "vocab": v}, device_id_type=MESH)
    for o in range(1, n_vocab):
        pl.semaphore_signal(barrier, inc=1, device_id={"dp": d, "vocab": lax.rem(v + o, n_vocab)}, device_id_type=MESH)
    pl.semaphore_wait(barrier, n_dp + n_vocab - 2)

    heads = ((th_ref, hid_t, wide), (sh_ref, hid_s, narrow))

    def region(hid, s, q, width):
        first = s * half
        if not isinstance(first, int):
            first = pl.multiple_of(first, half)
        return hid.at[pl.ds(first, half), pl.ds(pl.multiple_of(q * width, LANES), width)]

    y_to, core_to = row // 2, lax.rem(row, 2)
    k_of, rel = lax.rem(y - y_to + n_y, n_y), lax.rem(core + core_to, 2)
    local = row == d

    def source_copies(k, h):
        s = (k - 1) * 4 + h * 2 + rel if k else (n_y - 1) * 4 + rel * 2 + h
        return [
            remote(
                src.at[pl.ds(h * half, half), :], region(hid, s, col, width),
                src_send.at[h, e], g_recv.at[col, s, e], row, v,
            )
            for e, (src, hid, width) in enumerate(heads)
        ]

    def own_copies(h):
        s = (n_y - 1) * 4 + h
        return [
            pltpu.make_async_copy(
                src.at[pl.ds(h * half, half), :], region(hid, s, col, width), g_recv.at[col, s, e]
            )
            for e, (src, hid, width) in enumerate(heads)
        ]

    for k in range(n_y):

        @pl.when((k_of == k) & jnp.logical_not(local))
        def _(k=k):
            for h in range(2):
                for copy in source_copies(k, h):
                    copy.start()

    @pl.when(local)
    def _():
        for h in range(2):
            for copy in own_copies(h):
                copy.start()

    def arrived(s, q):
        for e, (_, hid, width) in enumerate(heads):
            at = region(hid, s, q, width)
            pltpu.make_async_copy(at, at, g_recv.at[q, s, e]).wait()

    up, down = (row >= d) & (row + 1 < n_dp), (row <= d) & (row > 0)

    def forwards(s, e):
        _, hid, width = heads[e]
        at = region(hid, s, col, width)
        recv = g_recv.at[col, s, e]
        peers = [
            remote(at, at, g_send.at[s, e, 1 + o], recv, d, row * per + lax.rem(col + o, per)) for o in range(1, per)
        ]
        return (
            remote(at, at, g_send.at[s, e, 0], recv, d, lax.rem(v + per, n_vocab)),
            remote(at, at, g_send.at[s, e, 1], recv, d, lax.rem(v + n_vocab - per, n_vocab)),
            peers,
        )

    def relay(s):
        for e, (_, hid, width) in enumerate(heads):
            at = region(hid, s, col, width)
            pltpu.make_async_copy(at, at, g_recv.at[col, s, e]).wait()
            above, below, peers = forwards(s, e)

            @pl.when(up)
            def _():
                above.start()

            @pl.when(down)
            def _():
                below.start()

            for copy in peers:
                copy.start()

    def peers_arrived(s):
        for o in range(1, per):
            arrived(s, lax.rem(col + o, per))

    away = jnp.abs(row - d)

    def matmul(g, first, rows):
        slot, at = lax.rem(g, SLOTS), lax.rem(g, 2)
        where = pl.ds(first, rows)
        part[at, 0, pl.ds(0, rows), :] = jnp.dot(hid_t[where, :], wt[slot], preferred_element_type=jnp.float32)
        part[at, 1, pl.ds(0, rows), :] = jnp.dot(hid_s[where, :], ws[slot], preferred_element_type=jnp.float32)

    partner = d + 1 - 2 * core

    def pair_copy_a(g):
        at = lax.rem(g, 2)
        return remote(
            part.at[at, :, pl.ds(half, half), :], pair_a.at[g], d_send.at[at], d_recv.at[g], partner, v
        )

    def pair_copy_b(i):
        at = lax.rem(n_a + i, 2)
        return remote(
            part.at[at, :, pl.ds(tok, tok), :], pair_b.at[i], d_send.at[at], d_recv.at[n_a + i], partner, v
        )

    def code_copies(g):
        k = g // (2 * n) + 1
        to = lax.rem(y + k, n_y) * 2 + core
        return (
            remote(code_out.at[g], code_in.at[g], y_send.at[g, 0], y_recv.at[g, 0], to, v),
            remote(top_out.at[g], top_in.at[g], y_send.at[g, 1], y_recv.at[g, 1], to, v),
        )

    def code_start(g):
        for copy in code_copies(g):
            copy.start()

    def finish_a(g):
        at = lax.rem(g, 2)
        pair_copy_a(g).wait()
        tops = []
        for e in range(2):
            code, top = encode(part[at, e, pl.ds(0, half), :] + pair_a[g, e])
            code_out[g, e] = code
            tops.append(top)
        tops = jnp.broadcast_to(jnp.concatenate(tops, axis=0), (tok, LANES))
        top_out[g] = tops.T[:8]

    def finish_b(i):
        at = lax.rem(n_a + i, 2)
        pair_copy_b(i).wait()
        for p in range(passes):
            for copy in code_copies(p * n + i):
                copy.wait_recv()
        for h in range(2):
            rows = pl.ds(h * half, half)
            t, s = (part[at, e, rows, :] + pair_b[i, e, rows, :] for e in range(2))
            for k in range(1, n_y):
                g = ((k - 1) * 2 + h) * n + i
                scale = (jnp.broadcast_to(top_in[g][:1], (LANES, tok)).T) * (1.0 / SPAN)
                blocks = cols // LANES
                t = t + decode(code_in[g, 0], jnp.concatenate([scale[:half]] * blocks, axis=1))
                s = s + decode(code_in[g, 1], jnp.concatenate([scale[half:]] * blocks, axis=1))
            ts = [t[:, b * LANES : (b + 1) * LANES] for b in range(cols // LANES)]
            ss = [s[:, b * LANES : (b + 1) * LANES] for b in range(cols // LANES)]
            t_old, s_old = run[0, rows, :], run[1, rows, :]
            t_top = functools.reduce(jnp.maximum, ts, t_old)
            s_top = functools.reduce(jnp.maximum, ss, s_old)
            t_fix = jnp.exp(t_old - t_top)
            t_sum, w_sum = run[2, rows, :] * t_fix, run[3, rows, :] * t_fix
            s_sum = run[4, rows, :] * jnp.exp(s_old - s_top)
            for tb, sb in zip(ts, ss):
                e = jnp.exp(tb - t_top)
                t_sum = t_sum + e
                w_sum = w_sum + e * (tb - sb)
                s_sum = s_sum + jnp.exp(sb - s_top)
            run[0, rows, :], run[1, rows, :] = t_top, s_top
            run[2, rows, :], run[3, rows, :], run[4, rows, :] = t_sum, w_sum, s_sum

    run[pl.ds(0, 2)] = jnp.full((2, tok, LANES), -jnp.inf, jnp.float32)
    run[pl.ds(2, 3)] = jnp.zeros((3, tok, LANES), jnp.float32)

    for s in range(2):
        relay(s)

    def step_a(g, _):
        @pl.when(g >= 1)
        def _():
            pair_copy_a(g - 1).start()

        @pl.when(g >= 2)
        def _():
            code_start(g - 2)

        for s in range(2, n_slots):
            deadline = min(s // 2, passes) * n - 1
            usual = 1 + SPACE * (s - 2) + HOP * away

            @pl.when(g == jnp.minimum(usual, deadline))
            def _(s=s):
                relay(s)

        p = g // n

        @pl.when(lax.rem(g, n) == 0)
        def _():
            for q in range(passes):

                @pl.when(p == q)
                def _(q=q):
                    peers_arrived(2 * q)
                    peers_arrived(2 * q + 1)

        for copy in weight_copies(g):
            copy.wait()
        weights_start(g + SLOTS - 1)
        matmul(g, pl.multiple_of(p * tok, tok), tok)

        @pl.when(g >= 1)
        def _():
            finish_a(g - 1)

        return 0

    lax.fori_loop(0, n_a, step_a, 0)

    pair_copy_a(jnp.int32(n_a - 1)).start()
    code_start(jnp.int32(n_a - 2))
    for s in range(4 * (n_y - 1), n_slots):
        peers_arrived(s)

    def step_b(i, _):
        g = n_a + i

        @pl.when(i >= 1)
        def _():
            pair_copy_b(i - 1).start()

        @pl.when(i == 1)
        def _():
            code_start(jnp.int32(n_a - 1))

        for copy in weight_copies(g):
            copy.wait()

        @pl.when(g + SLOTS - 1 < total)
        def _():
            weights_start(g + SLOTS - 1)

        matmul(g, passes * tok, 2 * tok)

        @pl.when(i == 0)
        def _():
            finish_a(jnp.int32(n_a - 1))

        @pl.when(i >= 1)
        def _():
            finish_b(i - 1)

        return 0

    lax.fori_loop(0, n, step_b, 0)
    pair_copy_b(jnp.int32(n - 1)).start()
    finish_b(jnp.int32(n - 1))

    t_lane, s_lane = run[0], run[1]
    t_top = jnp.max(t_lane, axis=1, keepdims=True)
    s_top = jnp.max(s_lane, axis=1, keepdims=True)
    t_fix = jnp.exp(t_lane - t_top)
    t_sum = jnp.sum(run[2] * t_fix, axis=1, keepdims=True)
    w_sum = jnp.sum(run[3] * t_fix, axis=1, keepdims=True)
    s_sum = jnp.sum(run[4] * jnp.exp(s_lane - s_top), axis=1, keepdims=True)
    lane = lax.broadcasted_iota(jnp.int32, (tok, LANES), 1)
    table = jnp.zeros((tok, LANES), jnp.float32)
    for i, stat in enumerate((t_top, s_top, t_sum, w_sum, s_sum)):
        table = jnp.where(lane == i, stat, table)
    table = table.T[:8]
    st_out[...] = table
    st_in[v] = table

    for k in range(n_y):

        @pl.when((k_of == k) & jnp.logical_not(local))
        def _(k=k):
            for h in range(2):
                for copy in source_copies(k, h):
                    copy.wait_send()

    def drain_codes(g, _):
        for copy in code_copies(g):
            copy.wait_send()
        return 0

    lax.fori_loop(0, n_a, drain_codes, 0)

    for s in range(n_slots):
        for e in range(2):
            above, below, peers = forwards(s, e)

            @pl.when(up)
            def _():
                above.wait_send()

            @pl.when(down)
            def _():
                below.wait_send()

            for copy in peers:
                copy.wait_send()

    def stat_copy(to, holder):
        return remote(st_out, st_in.at[holder], st_send.at[to], st_recv.at[holder], d, to)

    others = [lax.rem(v + o, n_vocab) for o in range(1, n_vocab)]
    for o in others:
        stat_copy(o, v).start()
    for o in others:
        stat_copy(v, o).wait_recv()

    def field(holder, i):
        return st_in[holder, pl.ds(i, 1), :]

    t_max = functools.reduce(jnp.maximum, [field(q, 0) for q in range(n_vocab)])
    s_max = functools.reduce(jnp.maximum, [field(q, 1) for q in range(n_vocab)])
    t_total = weighted = s_total = jnp.zeros((1, tok), jnp.float32)
    for q in range(n_vocab):
        scale = jnp.exp(field(q, 0) - t_max)
        t_total = t_total + scale * field(q, 2)
        weighted = weighted + scale * field(q, 3)
        s_total = s_total + jnp.exp(field(q, 1) - s_max) * field(q, 4)
    kl = weighted / t_total - (t_max + jnp.log(t_total)) + (s_max + jnp.log(s_total))
    kl_ref[...] = kl
    mine = jnp.broadcast_to(jnp.sum(kl, axis=1, keepdims=True), (8, LANES))
    ls_out[...] = mine
    ls_in[d] = mine
    for o in others:
        stat_copy(o, v).wait_send()

    def loss_copy(to, holder):
        return remote(ls_out, ls_in.at[holder], ls_send.at[to], ls_recv.at[holder], to, v)

    others = [lax.rem(d + o, n_dp) for o in range(1, n_dp)]
    for o in others:
        loss_copy(o, d).start()
    for o in others:
        loss_copy(d, o).wait_recv()
    loss = functools.reduce(jnp.add, [ls_in[q] for q in range(n_dp)]) / (tok * n_dp)
    loss_ref[...] = loss[:1, :1]
    for o in others:
        loss_copy(o, d).wait_send()


def shards(teacher_hidden, student_hidden, teacher_weight, student_weight):
    n_dp, n_vocab = lax.axis_size("dp"), lax.axis_size("vocab")
    tok, wide = teacher_hidden.shape
    narrow = student_hidden.shape[1]
    deep, local_cols = teacher_weight.shape
    shallow = student_weight.shape[0]
    cols = min(512, local_cols)
    n, n_y, per, half = local_cols // cols, n_dp // 2, n_vocab // n_dp, tok // 2
    n_a = 2 * (n_y - 1) * n
    slots = 4 * n_y
    bf16, f32, dma = jnp.bfloat16, jnp.float32, pltpu.SemaphoreType.DMA
    hbm = pl.BlockSpec(memory_space=pl.ANY)
    vmem = pl.BlockSpec(memory_space=pltpu.VMEM)
    kl, loss = pl.pallas_call(
        functools.partial(kernel, n_dp, n_vocab, cols),
        out_shape=(jax.ShapeDtypeStruct((1, tok), f32), jax.ShapeDtypeStruct((1, 1), f32)),
        in_specs=[hbm] * 4,
        out_specs=(vmem, vmem),
        scratch_shapes=[
            pltpu.VMEM((n_dp * tok, deep), bf16),
            pltpu.VMEM((n_dp * tok, shallow), bf16),
            pltpu.VMEM((SLOTS, deep, cols), bf16),
            pltpu.VMEM((SLOTS, shallow, cols), bf16),
            pltpu.VMEM((2, 2, 2 * tok, cols), f32),
            pltpu.VMEM((n_a, 2, half, cols), f32),
            pltpu.VMEM((n, 2, tok, cols), f32),
            pltpu.VMEM((n_a, 2, half, cols), bf16),
            pltpu.VMEM((n_a, 2, half, cols), bf16),
            pltpu.VMEM((n_a, 8, tok), f32),
            pltpu.VMEM((n_a, 8, tok), f32),
            pltpu.VMEM((5, tok, LANES), f32),
            pltpu.VMEM((8, tok), f32),
            pltpu.VMEM((n_vocab, 8, tok), f32),
            pltpu.VMEM((8, LANES), f32),
            pltpu.VMEM((n_dp, 8, LANES), f32),
            dma((per, slots, 2)),
            dma((slots, 2, per + 1)),
            dma((2, 2)),
            dma((SLOTS, 2)),
            dma((2,)),
            dma((n_a + n,)),
            dma((n_a, 2)),
            dma((n_a, 2)),
            dma((n_vocab,)),
            dma((n_vocab,)),
            dma((n_dp,)),
            dma((n_dp,)),
        ],
        compiler_params=pltpu.CompilerParams(
            collective_id=0, has_side_effects=True, vmem_limit_bytes=64 * 1024 * 1024 - 65536
        ),
    )(teacher_hidden, student_hidden, teacher_weight, student_weight)
    return kl.reshape(tok), loss.reshape(())


def solution(mesh):
    in_specs = (P("dp", "vocab"), P("dp", "vocab"), P("dp", "vocab"), P("dp", "vocab"))
    out_specs = (P("dp"), P())
    return jax.shard_map(shards, mesh=mesh, in_specs=in_specs, out_specs=out_specs, check_vma=False)
```

time: 354 us -> 156 us (0.44)
  Pallas kernels: 0 us -> 152 us
  waiting for transfers between devices: 115 us -> 0 us
  blocking collectives: 89.4 us -> 0 us
  matrix products: 70.4 us -> 0 us
  other arithmetic: 27.3 us -> 0 us
  starting transfers between devices: 21.7 us -> 0 us
  between operations: 16.4 us -> 2.4 us
  local copies, waits for them, and re-layouts: 13.6 us -> 1.11 us
    pallas_call x0 -> x1, Pallas kernels: none -> 152 us  [shards(): pl.pallas_call(functools.partial(kernel, n_dp, n_vocab, cols), out_shape=...]
    dot_general x8 -> x0, matrix products: 70.4 us -> none  [head(): waiting.append(jnp.dot(rows, piece, preferred_element_type=jnp.float32))]
    all_gather x1 -> x0, blocking collectives: 64.5 us -> none  [shards(): lax.all_gather(jnp.stack([t_top, s_top, t_sum, w_sum, s_sum]), ('dp', 'vo...]
    ppermute x24 -> x0, waiting for transfers between devices: 57.2 us -> none  [the longest x8 29.9 us: exchange(): lax.ppermute(code, 'dp', perm)]
    all_gather x2 -> x0, waiting for transfers between devices: 47.3 us -> none  [gather(): full = lax.all_gather(piece, 'vocab', axis=1, tiled=True)]
    all_to_all x1 -> x0, blocking collectives: 24.9 us -> none  [shards(): lax.all_to_all(both, 'vocab', split_axis=0, concat_axis=0, tiled=True)]
    ppermute x24 -> x0, starting transfers between devices: 18.1 us -> none  [the longest x8 8.37 us: exchange(): lax.ppermute(top, 'dp', perm)]
    all_to_all x1 -> x0, waiting for transfers between devices: 10.1 us -> none  [shards(): both = lax.all_to_all(both, 'dp', split_axis=0, concat_axis=0, tiled=True)]
  transfers between devices with their start and end apart: 27 -> 0, of which waited for: 11 -> 0; matrix products, arithmetic and copies ran while one was open for 26% -> 0% of each run, Pallas kernels for 0% -> 0%
where the time goes in v1:
time: 156 us
  Pallas kernels  152 us (97%)
  between operations  2.4 us (2%)
    pallas_call x1, Pallas kernels, shards(): pl.pallas_call(functools.partial(kernel, n_dp, n_vocab, cols), out_shape=...  152 us

profile of v1, /device:TPU:0, one launch (start us, length us, event | category | flops | bytes accessed | tf_op | source)
XLA Modules:
  0.0 155.5 jit_solution(8454249900568946424)
XLA Ops:
  0.6 152.0 %shard_map.59 = (f32[1,128]{1,0:T(1,128)}, f32[1,1]{1,0:T(1,128)}) custom-call(bf16[128,2048]{1,0:T(8,128)(2,1)} %th_ref.1, bf16[128,512]{1,0:T(8,128)(2,1)} %sh_ref.1, bf16[4096,8192]{1,0:T(8,128)(2,1)} %tw_ref.1, bf16[1024,8192]{1,0:T(8,128)(2,1)} %sw_ref.1), custom_call_target="tpu_custom_call" | custom-call | tf_op jit(solution)/shard_map/pallas_call | solution.py:430
  152.6 1.1 copy.8

commit v2 on v1

v2 whole, which is shorter than its diff:
```python
import functools

import jax
import jax.numpy as jnp
from jax import lax
from jax.experimental import pallas as pl
from jax.experimental.pallas import tpu as pltpu
from jax.sharding import PartitionSpec as P

MESH = pl.DeviceIdType.MESH
SPAN = 240.0
LANES = 128
SLOTS = 3
HOP = 2
SPACE = 4
LATE = 14


def encode(block):
    mag = jnp.abs(block)
    top = jnp.max(mag, axis=1, keepdims=True)
    step = jnp.where(top > 0, SPAN / jnp.where(top > 0, top, 1.0), 0.0)
    power = jnp.exp2(mag * step - 0.5 * SPAN)
    return jnp.where(block < 0, -power, power).astype(jnp.bfloat16), top


def decode(code, scale):
    value = code.astype(jnp.float32)
    mag = (jnp.log2(jnp.abs(value)) + 0.5 * SPAN) * scale
    return jnp.where(value < 0, -mag, mag)


def kernel(
    n_dp, n_vocab, cols,
    th_ref, sh_ref, tw_ref, sw_ref, kl_ref, loss_ref,
    hid_t, hid_s, wt, ws, part, pair_q, pair_r, pair_b, out_q, in_q, out_r, in_r, top_out_q, top_in_q, top_out_r,
    top_in_r, run, st_out, st_in, ls_out, ls_in, kl_out, loss_out,
    g_recv, g_send, src_send, w_sem, d_send, d_recv, y_send, y_recv, st_send, st_recv, ls_send, ls_recv, out_sem,
):
    tok, wide = th_ref.shape
    narrow = sh_ref.shape[1]
    quarter, half = tok // 4, tok // 2
    n_y = n_dp // 2
    per = n_vocab // n_dp
    n = tw_ref.shape[1] // cols
    phases = [(k, early) for k in range(1, n_y) for early in (True, False)] + [(0, False)]
    total = len(phases) * n
    n_far = 8 * (n_y - 1)
    n_slots = n_far + 4

    d, v = lax.axis_index("dp"), lax.axis_index("vocab")
    y, core = d // 2, lax.rem(d, 2)
    row, col = v // per, lax.rem(v, per)

    def remote(src, dst, send, recv, dp, vocab):
        return pltpu.make_async_remote_copy(
            src_ref=src, dst_ref=dst, send_sem=send, recv_sem=recv,
            device_id={"dp": dp, "vocab": vocab}, device_id_type=MESH,
        )

    def weight_copies(g):
        at = pl.ds(pl.multiple_of(lax.rem(g, n) * cols, LANES), cols)
        slot = lax.rem(g, SLOTS)
        return (
            pltpu.make_async_copy(tw_ref.at[:, at], wt.at[slot], w_sem.at[slot, 0]),
            pltpu.make_async_copy(sw_ref.at[:, at], ws.at[slot], w_sem.at[slot, 1]),
        )

    def weights_start(g):
        for copy in weight_copies(g):
            copy.start()

    for g in range(SLOTS - 1):
        weights_start(jnp.int32(g))

    barrier = pltpu.get_barrier_semaphore()
    for o in range(1, n_dp):
        pl.semaphore_signal(barrier, inc=1, device_id={"dp": lax.rem(d + o, n_dp), "vocab": v}, device_id_type=MESH)
    for o in range(1, n_vocab):
        pl.semaphore_signal(barrier, inc=1, device_id={"dp": d, "vocab": lax.rem(v + o, n_vocab)}, device_id_type=MESH)
    with jax.named_scope("barrier"):
        pl.semaphore_wait(barrier, n_dp + n_vocab - 2)

    heads = ((th_ref, hid_t, wide), (sh_ref, hid_s, narrow))

    def place(s):
        if s >= n_far:
            rel, h = divmod(s - n_far, 2)
            return (n_y - 1) * 2 * tok + rel * tok + h * half, half, h * half
        k, at = divmod(s, 8)
        j, rel = divmod(at, 2)
        inside = rel * quarter if j == 0 else 2 * quarter + (3 * rel + j - 1) * quarter
        return k * 2 * tok + inside, quarter, j * quarter

    def slots_of(k, rel):
        if k:
            return [(k - 1) * 8 + j * 2 + rel for j in range(4)]
        return [n_far + rel * 2 + h for h in range(2)]

    def region(hid, s, q, width):
        first, size, _ = place(s)
        return hid.at[pl.ds(first, size), pl.ds(pl.multiple_of(q * width, LANES), width)]

    y_to, core_to = row // 2, lax.rem(row, 2)
    k_of, rel_of = lax.rem(y - y_to + n_y, n_y), lax.rem(core + core_to, 2)

    def source_copies(k, rel):
        out = []
        for i, s in enumerate(slots_of(k, rel)):
            _, size, first = place(s)
            for e, (src, hid, width) in enumerate(heads):
                piece, at, recv = src.at[pl.ds(first, size), :], region(hid, s, col, width), g_recv.at[col, s, e]
                if k or rel:
                    out.append(remote(piece, at, src_send.at[i, e], recv, row, v))
                else:
                    out.append(pltpu.make_async_copy(piece, at, recv))
        return out

    def each_source(act, local=True):
        for k in range(n_y):
            for rel in range(0 if k or local else 1, 2):

                @pl.when((k_of == k) & (rel_of == rel))
                def _(k=k, rel=rel):
                    for copy in source_copies(k, rel):
                        act(copy)

    each_source(lambda copy: copy.start())

    def arrived(s, q):
        for e, (_, hid, width) in enumerate(heads):
            at = region(hid, s, q, width)
            pltpu.make_async_copy(at, at, g_recv.at[q, s, e]).wait()

    up, down = (row >= d) & (row + 1 < n_dp), (row <= d) & (row > 0)

    def forwards(s, e):
        _, hid, width = heads[e]
        at = region(hid, s, col, width)
        recv = g_recv.at[col, s, e]
        peers = [
            remote(at, at, g_send.at[s, e, 1 + o], recv, d, row * per + lax.rem(col + o, per)) for o in range(1, per)
        ]
        return (
            remote(at, at, g_send.at[s, e, 0], recv, d, lax.rem(v + per, n_vocab)),
            remote(at, at, g_send.at[s, e, 1], recv, d, lax.rem(v + n_vocab - per, n_vocab)),
            peers,
        )

    def relay_wait(s, e):
        _, hid, width = heads[e]
        at = region(hid, s, col, width)
        pltpu.make_async_copy(at, at, g_recv.at[col, s, e]).wait()

    def relay_send(s, e):
        above, below, peers = forwards(s, e)

        @pl.when(up)
        def _():
            above.start()

        @pl.when(down)
        def _():
            below.start()

        for copy in peers:
            copy.start()

    def relay(s):
        for e in range(2):
            relay_wait(s, e)
            relay_send(s, e)

    def peers_arrived(s):
        for o in range(1, per):
            arrived(s, lax.rem(col + o, per))

    away = jnp.abs(row - d)
    moved, moved_far = jnp.minimum(away, 1), jnp.minimum(away // 2, 1)
    longest = 1 - jnp.minimum(jnp.minimum(d, n_dp - 1 - d), 1)

    def slots_in(f):
        k, early = phases[f]
        if k == 0:
            return range(n_far, n_slots)
        first = (k - 1) * 8
        return range(first, first + 2) if early else range(first + 2, first + 8)

    def relay_step(s):
        f = next(f for f in range(len(phases)) if s in slots_in(f))
        if s >= n_far:
            usual = LATE + SPACE * (s - n_far) + HOP * away
        else:
            j = (s % 8) // 2
            first = moved_far * (4 * j - 3 + 3 * (away - 2))
            other = moved * (4 * j + 2 * (away - 1)) + (1 - moved) * (-1 if s < 8 else 1)
            usual = (s // 8) * 2 * n + (longest * first + (1 - longest) * other if j else 0)
        return jnp.minimum(usual, max(f * n - 1, 0))

    def rows_of(f):
        k, early = phases[f]
        if k == 0:
            return (n_y - 1) * 2 * tok, tok
        return (k - 1) * 2 * tok + (0 if early else 2 * quarter), quarter if early else 3 * quarter

    def matmul(g, f):
        first, size = rows_of(f)
        slot, at = lax.rem(g, SLOTS), lax.rem(g, 2)
        x_t, x_s = hid_t[first : first + 2 * size, :], hid_s[first : first + 2 * size, :]
        part[at, 0, pl.ds(0, 2 * size), :] = jnp.dot(x_t, wt[slot], preferred_element_type=jnp.float32)
        part[at, 1, pl.ds(0, 2 * size), :] = jnp.dot(x_s, ws[slot], preferred_element_type=jnp.float32)

    partner = d + 1 - 2 * core

    def pair_buffer(f, i):
        k, early = phases[f]
        if k == 0:
            return pair_b.at[i]
        return (pair_q if early else pair_r).at[(k - 1) * n + i]

    def pair_copy(f, i):
        g = f * n + i
        at, size = lax.rem(g, 2), rows_of(f)[1]
        return remote(
            part.at[at, :, pl.ds(size, size), :], pair_buffer(f, i), d_send.at[at], d_recv.at[g], partner, v
        )

    def code_copies(f, i):
        k, early = phases[f]
        at, g = (k - 1) * n + i, f * n + i
        to = lax.rem(y + k, n_y) * 2 + core
        code_out, code_in = (out_q, in_q) if early else (out_r, in_r)
        top_out, top_in = (top_out_q, top_in_q) if early else (top_out_r, top_in_r)
        return (
            remote(code_out.at[at], code_in.at[at], y_send.at[g, 0], y_recv.at[g, 0], to, v),
            remote(top_out.at[at], top_in.at[at], y_send.at[g, 1], y_recv.at[g, 1], to, v),
        )

    def code_start(f, i):
        if phases[f][0]:
            for copy in code_copies(f, i):
                copy.start()

    def finish_far(f, i):
        k, early = phases[f]
        at, size = (k - 1) * n + i, rows_of(f)[1]
        slot = lax.rem(f * n + i, 2)
        pair_copy(f, i).wait()
        code_out, top_out, pair = (out_q, top_out_q, pair_q) if early else (out_r, top_out_r, pair_r)
        tops = []
        for e in range(2):
            code, top = encode(part[slot, e, pl.ds(0, size), :] + pair[at, e])
            code_out[at, e] = code
            tops.append(jnp.broadcast_to(top, (size, LANES)))
        spare = top_out.shape[2] - 2 * size
        tops = jnp.concatenate(tops + [jnp.zeros((spare, LANES), jnp.float32)], axis=0)
        top_out[at] = tops.T[:8]

    def absorb(first, size, t, s):
        rows = pl.ds(first, size)
        ts = [t[:, b * LANES : (b + 1) * LANES] for b in range(cols // LANES)]
        ss = [s[:, b * LANES : (b + 1) * LANES] for b in range(cols // LANES)]
        t_old, s_old = run[0, rows, :], run[1, rows, :]
        t_top = functools.reduce(jnp.maximum, ts, t_old)
        s_top = functools.reduce(jnp.maximum, ss, s_old)
        t_fix = jnp.exp(t_old - t_top)
        t_sum, w_sum = run[2, rows, :] * t_fix, run[3, rows, :] * t_fix
        s_sum = run[4, rows, :] * jnp.exp(s_old - s_top)
        for tb, sb in zip(ts, ss):
            e = jnp.exp(tb - t_top)
            t_sum = t_sum + e
            w_sum = w_sum + e * (tb - sb)
            s_sum = s_sum + jnp.exp(sb - s_top)
        run[0, rows, :], run[1, rows, :] = t_top, s_top
        run[2, rows, :], run[3, rows, :], run[4, rows, :] = t_sum, w_sum, s_sum

    def finish_near(f, i):
        slot = lax.rem(f * n + i, 2)
        pair_copy(f, i).wait()
        for o in range(len(phases) - 1):
            for copy in code_copies(o, i):
                with jax.named_scope("ywait"):
                    copy.wait_recv()
        for early in (True, False):
            first, size = (0, quarter) if early else (quarter, 3 * quarter)
            code_in, top_in = (in_q, top_in_q) if early else (in_r, top_in_r)
            t, s = (
                part[slot, e, pl.ds(first, size), :] + pair_b[i, e, pl.ds(first, size), :] for e in range(2)
            )
            for k in range(1, n_y):
                at = (k - 1) * n + i
                scale = (jnp.broadcast_to(top_in[at][:1], (LANES, top_in.shape[2])).T) * (1.0 / SPAN)
                blocks = cols // LANES
                t = t + decode(code_in[at, 0], jnp.concatenate([scale[:size]] * blocks, axis=1))
                s = s + decode(code_in[at, 1], jnp.concatenate([scale[size : 2 * size]] * blocks, axis=1))
            absorb(first, size, t, s)

    def finish(f, i):
        if phases[f][0]:
            finish_far(f, i)
        else:
            finish_near(f, i)

    run[pl.ds(0, 2)] = jnp.full((2, tok, LANES), -jnp.inf, jnp.float32)
    run[pl.ds(2, 3)] = jnp.zeros((3, tok, LANES), jnp.float32)

    for f in range(len(phases)):

        def step(i, _, f=f):
            g = f * n + i

            @pl.when(i >= 1)
            def _():
                pair_copy(f, i - 1).start()

            @pl.when(i >= 2)
            def _():
                code_start(f, i - 2)

            if f:

                @pl.when(i == 0)
                def _():
                    pair_copy(f - 1, jnp.int32(n - 1)).start()
                    code_start(f - 1, jnp.int32(n - 2))

                @pl.when(i == 1)
                def _():
                    code_start(f - 1, jnp.int32(n - 1))

            if f == 0:
                @pl.when((i == 1) & (away == 0) & (longest == 0))
                def _():
                    with jax.named_scope("relay"):
                        for act in (relay_wait, relay_send):
                            for s in range(2, 8):
                                for e in range(2):
                                    act(s, e)

            if f < len(phases) - 1:
                for s in range(slots_in(f).start, n_slots):

                    @pl.when(g == relay_step(s))
                    def _(s=s):
                        with jax.named_scope("relay"):
                            relay(s)

            @pl.when(i == 0)
            def _():
                with jax.named_scope("peers"):
                    for s in slots_in(f):
                        peers_arrived(s)

            with jax.named_scope("wwait"):
                for copy in weight_copies(g):
                    copy.wait()

            @pl.when(g + SLOTS - 1 < total)
            def _():
                weights_start(g + SLOTS - 1)

            with jax.named_scope("mm"):
                matmul(g, f)

            @pl.when(i >= 1)
            def _():
                with jax.named_scope("finish"):
                    finish(f, i - 1)

            if f:

                @pl.when(i == 0)
                def _():
                    with jax.named_scope("finish"):
                        finish(f - 1, jnp.int32(n - 1))

            return 0

        lax.fori_loop(0, n, step, 0)

    last = len(phases) - 1
    pair_copy(last, jnp.int32(n - 1)).start()
    finish(last, jnp.int32(n - 1))

    t_lane, s_lane = run[0], run[1]
    t_top = jnp.max(t_lane, axis=1, keepdims=True)
    s_top = jnp.max(s_lane, axis=1, keepdims=True)
    t_fix = jnp.exp(t_lane - t_top)
    t_sum = jnp.sum(run[2] * t_fix, axis=1, keepdims=True)
    w_sum = jnp.sum(run[3] * t_fix, axis=1, keepdims=True)
    s_sum = jnp.sum(run[4] * jnp.exp(s_lane - s_top), axis=1, keepdims=True)
    lane = lax.broadcasted_iota(jnp.int32, (tok, LANES), 1)
    table = jnp.zeros((tok, LANES), jnp.float32)
    for i, stat in enumerate((t_top, s_top, t_sum, w_sum, s_sum)):
        table = jnp.where(lane == i, stat, table)
    table = table.T[:8]
    st_out[...] = table
    st_in[v] = table

    each_source(lambda copy: copy.wait_send(), local=False)

    for f in range(last):

        def drain_codes(i, _, f=f):
            for copy in code_copies(f, i):
                copy.wait_send()
            return 0

        lax.fori_loop(0, n, drain_codes, 0)

    for s in range(n_slots):
        for e in range(2):
            above, below, peers = forwards(s, e)

            @pl.when(up)
            def _():
                above.wait_send()

            @pl.when(down)
            def _():
                below.wait_send()

            for copy in peers:
                copy.wait_send()

    def stat_copy(to, holder):
        return remote(st_out, st_in.at[holder], st_send.at[to], st_recv.at[holder], d, to)

    others = [lax.rem(v + o, n_vocab) for o in range(1, n_vocab)]
    for o in others:
        stat_copy(o, v).start()
    with jax.named_scope("statwait"):
        for o in others:
            stat_copy(v, o).wait_recv()

    def field(holder, i):
        return st_in[holder, pl.ds(i, 1), :]

    t_max = functools.reduce(jnp.maximum, [field(q, 0) for q in range(n_vocab)])
    s_max = functools.reduce(jnp.maximum, [field(q, 1) for q in range(n_vocab)])
    t_total = weighted = s_total = jnp.zeros((1, tok), jnp.float32)
    for q in range(n_vocab):
        scale = jnp.exp(field(q, 0) - t_max)
        t_total = t_total + scale * field(q, 2)
        weighted = weighted + scale * field(q, 3)
        s_total = s_total + jnp.exp(field(q, 1) - s_max) * field(q, 4)
    kl = weighted / t_total - (t_max + jnp.log(t_total)) + (s_max + jnp.log(s_total))
    kl_out[...] = kl
    mine = jnp.broadcast_to(jnp.sum(kl, axis=1, keepdims=True), (8, LANES))
    ls_out[...] = mine
    ls_in[d] = mine
    for o in others:
        stat_copy(o, v).wait_send()

    def loss_copy(to, holder):
        return remote(ls_out, ls_in.at[holder], ls_send.at[to], ls_recv.at[holder], to, v)

    others = [lax.rem(d + o, n_dp) for o in range(1, n_dp)]
    for o in others:
        loss_copy(o, d).start()
    kl_write = pltpu.make_async_copy(kl_out, kl_ref, out_sem.at[0])
    kl_write.start()
    with jax.named_scope("losswait"):
        for o in others:
            loss_copy(d, o).wait_recv()
    loss = functools.reduce(jnp.add, [ls_in[q] for q in range(n_dp)]) / (tok * n_dp)
    loss_out[...] = loss[:1, :1]
    for o in others:
        loss_copy(o, d).wait_send()
    loss_write = pltpu.make_async_copy(loss_out, loss_ref, out_sem.at[1])
    loss_write.start()
    loss_write.wait()
    kl_write.wait()


def shards(teacher_hidden, student_hidden, teacher_weight, student_weight):
    n_dp, n_vocab = lax.axis_size("dp"), lax.axis_size("vocab")
    tok, wide = teacher_hidden.shape
    narrow = student_hidden.shape[1]
    deep, local_cols = teacher_weight.shape
    shallow = student_weight.shape[0]
    cols = min(512, local_cols)
    n, n_y, per = local_cols // cols, n_dp // 2, n_vocab // n_dp
    few, many = tok // 4, 3 * tok // 4
    far = (n_y - 1) * n
    slots = 8 * (n_y - 1) + 4
    steps = 2 * far + n
    top_few, top_many = (-(-2 * rows // LANES) * LANES for rows in (few, many))
    bf16, f32, dma = jnp.bfloat16, jnp.float32, pltpu.SemaphoreType.DMA
    hbm = pl.BlockSpec(memory_space=pl.ANY)
    kl, loss = pl.pallas_call(
        functools.partial(kernel, n_dp, n_vocab, cols),
        out_shape=(jax.ShapeDtypeStruct((1, tok), f32), jax.ShapeDtypeStruct((1, 1), f32)),
        in_specs=[hbm] * 4,
        out_specs=(hbm, hbm),
        scratch_shapes=[
            pltpu.VMEM((n_dp * tok, deep), bf16),
            pltpu.VMEM((n_dp * tok, shallow), bf16),
            pltpu.VMEM((SLOTS, deep, cols), bf16),
            pltpu.VMEM((SLOTS, shallow, cols), bf16),
            pltpu.VMEM((2, 2, 2 * tok, cols), f32),
            pltpu.VMEM((far, 2, few, cols), f32),
            pltpu.VMEM((far, 2, many, cols), f32),
            pltpu.VMEM((n, 2, tok, cols), f32),
            pltpu.VMEM((far, 2, few, cols), bf16),
            pltpu.VMEM((far, 2, few, cols), bf16),
            pltpu.VMEM((far, 2, many, cols), bf16),
            pltpu.VMEM((far, 2, many, cols), bf16),
            pltpu.VMEM((far, 8, top_few), f32),
            pltpu.VMEM((far, 8, top_few), f32),
            pltpu.VMEM((far, 8, top_many), f32),
            pltpu.VMEM((far, 8, top_many), f32),
            pltpu.VMEM((5, tok, LANES), f32),
            pltpu.VMEM((8, tok), f32),
            pltpu.VMEM((n_vocab, 8, tok), f32),
            pltpu.VMEM((8, LANES), f32),
            pltpu.VMEM((n_dp, 8, LANES), f32),
            pltpu.VMEM((1, tok), f32),
            pltpu.VMEM((1, 1), f32),
            dma((per, slots, 2)),
            dma((slots, 2, per + 1)),
            dma((4, 2)),
            dma((SLOTS, 2)),
            dma((2,)),
            dma((steps,)),
            dma((2 * far, 2)),
            dma((2 * far, 2)),
            dma((n_vocab,)),
            dma((n_vocab,)),
            dma((n_dp,)),
            dma((n_dp,)),
            dma((2,)),
        ],
        compiler_params=pltpu.CompilerParams(
            collective_id=0, has_side_effects=True, vmem_limit_bytes=64 * 1024 * 1024 - 65536
        ),
    )(teacher_hidden, student_hidden, teacher_weight, student_weight)
    return kl.reshape(tok), loss.reshape(())


def solution(mesh):
    in_specs = (P("dp", "vocab"), P("dp", "vocab"), P("dp", "vocab"), P("dp", "vocab"))
    out_specs = (P("dp"), P())
    return jax.shard_map(shards, mesh=mesh, in_specs=in_specs, out_specs=out_specs, check_vma=False)
```

time: 156 us -> 149 us (0.955)
  Pallas kernels: 152 us -> 145 us
    pallas_call x1, Pallas kernels: 152 us -> 145 us  [shards(): pl.pallas_call(functools.partial(kernel, n_dp, n_vocab, cols), out_shape=...]
where the time goes in v2:
time: 149 us
  Pallas kernels  145 us (97%)
  between operations  2.4 us (2%)
    pallas_call x1, Pallas kernels, shards(): pl.pallas_call(functools.partial(kernel, n_dp, n_vocab, cols), out_shape=...  145 us

profile of v2, /device:TPU:0, one launch (start us, length us, event | category | flops | bytes accessed | tf_op | source)
XLA Modules:
  0.0 148.5 jit_solution(6453468791364520558)
XLA Ops:
  0.6 145.0 %shard_map.59 = (f32[1,128]{1,0:T(1,128)}, f32[1,1]{1,0:T(1,128)}) custom-call(bf16[128,2048]{1,0:T(8,128)(2,1)} %th_ref.1, bf16[128,512]{1,0:T(8,128)(2,1)} %sh_ref.1, bf16[4096,8192]{1,0:T(8,128)(2,1)} %tw_ref.1, bf16[1024,8192]{1,0:T(8,128)(2,1)} %sw_ref.1), custom_call_target="tpu_custom_call" | custom-call | tf_op jit(solution)/shard_map/pallas_call | solution.py:491
  145.7 1.1 copy.8

commit v3 on v2

--- a/solution.py
+++ b/solution.py
@@ -106,26 +106,23 @@
 
     def source_copies(k, rel):
         out = []
-        for i, s in enumerate(slots_of(k, rel)):
+        for s in slots_of(k, rel):
             _, size, first = place(s)
             for e, (src, hid, width) in enumerate(heads):
                 piece, at, recv = src.at[pl.ds(first, size), :], region(hid, s, col, width), g_recv.at[col, s, e]
                 if k or rel:
-                    out.append(remote(piece, at, src_send.at[i, e], recv, row, v))
+                    out.append(remote(piece, at, src_send.at[e], recv, row, v))
                 else:
                     out.append(pltpu.make_async_copy(piece, at, recv))
         return out
 
-    def each_source(act, local=True):
-        for k in range(n_y):
-            for rel in range(0 if k or local else 1, 2):
-
-                @pl.when((k_of == k) & (rel_of == rel))
-                def _(k=k, rel=rel):
-                    for copy in source_copies(k, rel):
-                        act(copy)
-
-    each_source(lambda copy: copy.start())
+    for k in range(n_y):
+        for rel in range(2):
+
+            @pl.when((k_of == k) & (rel_of == rel))
+            def _(k=k, rel=rel):
+                for copy in source_copies(k, rel):
+                    copy.start()
 
     def arrived(s, q):
         for e, (_, hid, width) in enumerate(heads):
@@ -139,11 +136,11 @@
         at = region(hid, s, col, width)
         recv = g_recv.at[col, s, e]
         peers = [
-            remote(at, at, g_send.at[s, e, 1 + o], recv, d, row * per + lax.rem(col + o, per)) for o in range(1, per)
+            remote(at, at, g_send.at[e, 1 + o], recv, d, row * per + lax.rem(col + o, per)) for o in range(1, per)
         ]
         return (
-            remote(at, at, g_send.at[s, e, 0], recv, d, lax.rem(v + per, n_vocab)),
-            remote(at, at, g_send.at[s, e, 1], recv, d, lax.rem(v + n_vocab - per, n_vocab)),
+            remote(at, at, g_send.at[e, 0], recv, d, lax.rem(v + per, n_vocab)),
+            remote(at, at, g_send.at[e, 1], recv, d, lax.rem(v + n_vocab - per, n_vocab)),
             peers,
         )
 
@@ -189,11 +186,11 @@
     def relay_step(s):
         f = next(f for f in range(len(phases)) if s in slots_in(f))
         if s >= n_far:
-            usual = LATE + SPACE * (s - n_far) + HOP * away
+            usual = LATE + SPACE * (s - n_far) + HOP * away - 3 * (1 - longest) * (1 - moved)
         else:
             j = (s % 8) // 2
-            first = moved_far * (4 * j - 3 + 3 * (away - 2))
-            other = moved * (4 * j + 2 * (away - 1)) + (1 - moved) * (-1 if s < 8 else 1)
+            first = moved_far * (4 * j - 3 + away - 2)
+            other = moved * (4 * j - 1 + 2 * (away - 1)) + (1 - moved) * (-1 if s < 8 else 1)
             usual = (s // 8) * 2 * n + (longest * first + (1 - longest) * other if j else 0)
         return jnp.minimum(usual, max(f * n - 1, 0))
 
@@ -229,11 +226,12 @@
         k, early = phases[f]
         at, g = (k - 1) * n + i, f * n + i
         to = lax.rem(y + k, n_y) * 2 + core
+        early = int(early)
         code_out, code_in = (out_q, in_q) if early else (out_r, in_r)
         top_out, top_in = (top_out_q, top_in_q) if early else (top_out_r, top_in_r)
         return (
-            remote(code_out.at[at], code_in.at[at], y_send.at[g, 0], y_recv.at[g, 0], to, v),
-            remote(top_out.at[at], top_in.at[at], y_send.at[g, 1], y_recv.at[g, 1], to, v),
+            remote(code_out.at[at], code_in.at[at], y_send.at[early, 0], y_recv.at[g, 0], to, v),
+            remote(top_out.at[at], top_in.at[at], y_send.at[early, 1], y_recv.at[g, 1], to, v),
         )
 
     def code_start(f, i):
@@ -397,31 +395,32 @@
     st_out[...] = table
     st_in[v] = table
 
-    each_source(lambda copy: copy.wait_send(), local=False)
-
-    for f in range(last):
-
-        def drain_codes(i, _, f=f):
-            for copy in code_copies(f, i):
-                copy.wait_send()
-            return 0
-
-        lax.fori_loop(0, n, drain_codes, 0)
-
-    for s in range(n_slots):
-        for e in range(2):
-            above, below, peers = forwards(s, e)
-
-            @pl.when(up)
-            def _():
-                above.wait_send()
-
-            @pl.when(down)
-            def _():
-                below.wait_send()
-
-            for copy in peers:
-                copy.wait_send()
+    def sent(ref, sem):
+        pltpu.make_async_copy(ref, ref, sem).wait()
+
+    @pl.when(row != d)
+    def _():
+        for e, (src, _, _) in enumerate(heads):
+            sent(src, src_send.at[e])
+
+    if n_y > 1:
+        for early, refs in enumerate(((out_r, top_out_r), (out_q, top_out_q))):
+            for e, ref in enumerate(refs):
+                sent(ref, y_send.at[early, e])
+
+    for e, (_, hid, width) in enumerate(heads):
+        passed = hid.at[:, pl.ds(pl.multiple_of(col * width, LANES), width)]
+
+        @pl.when(up)
+        def _():
+            sent(passed, g_send.at[e, 0])
+
+        @pl.when(down)
+        def _():
+            sent(passed, g_send.at[e, 1])
+
+        for o in range(1, per):
+            sent(passed, g_send.at[e, 1 + o])
 
     def stat_copy(to, holder):
         return remote(st_out, st_in.at[holder], st_send.at[to], st_recv.at[holder], d, to)
@@ -518,12 +517,12 @@
             pltpu.VMEM((1, tok), f32),
             pltpu.VMEM((1, 1), f32),
             dma((per, slots, 2)),
-            dma((slots, 2, per + 1)),
-            dma((4, 2)),
+            dma((2, per + 1)),
+            dma((2,)),
             dma((SLOTS, 2)),
             dma((2,)),
             dma((steps,)),
-            dma((2 * far, 2)),
+            dma((2, 2)),
             dma((2 * far, 2)),
             dma((n_vocab,)),
             dma((n_vocab,)),

time: 149 us -> 146 us (0.980)
  Pallas kernels: 145 us -> 143 us
    pallas_call x1, Pallas kernels: 145 us -> 143 us  [shards(): pl.pallas_call(functools.partial(kernel, n_dp, n_vocab, cols), out_shape=...]
where the time goes in v3:
time: 146 us
  Pallas kernels  143 us (98%)
  between operations  2.4 us (2%)
    pallas_call x1, Pallas kernels, shards(): pl.pallas_call(functools.partial(kernel, n_dp, n_vocab, cols), out_shape=...  143 us

profile of v3, /device:TPU:0, one launch (start us, length us, event | category | flops | bytes accessed | tf_op | source)
XLA Modules:
  0.0 146.2 jit_solution(12340468002212694634)
XLA Ops:
  0.6 142.6 %shard_map.59 = (f32[1,128]{1,0:T(1,128)}, f32[1,1]{1,0:T(1,128)}) custom-call(bf16[128,2048]{1,0:T(8,128)(2,1)} %th_ref.1, bf16[128,512]{1,0:T(8,128)(2,1)} %sh_ref.1, bf16[4096,8192]{1,0:T(8,128)(2,1)} %tw_ref.1, bf16[1024,8192]{1,0:T(8,128)(2,1)} %sw_ref.1), custom_call_target="tpu_custom_call" | custom-call | tf_op jit(solution)/shard_map/pallas_call | solution.py:490
  143.3 1.1 copy.8
